TPU v7x, 32 devices: a whole 2x2x4 slice. The times are simulated.
32 devices in a mesh: tm: 4 (over y, x), space: 8 (over z, core).
Axes of the slice: x: 2, y: 2, z: 4, core: 2. Of those that a mesh axis runs over, the one named last changes fastest.
Arguments:
- initial_state: float32 [16, 256, 256], P('space'), may hold values from -6 to 6
- capacity: float32 [16, 256, 256], P('space'), may hold values from 0.5 to 2
- source: float32 [16, 256, 256], P('space'), may hold values from -6 to 6
- control: float32 [4, 16], P('tm'), may hold values from -2 to 2
- segment_index: int32 [16, 256], P('space'), may hold values from 0 to 15
Outputs:
- slice_ends: float32 [4, 16, 256, 256], P('tm', 'space')
All inputs are finite; a program needn't handle non-finite values.
Results may differ from a plain program's by a relative error of at most 0.0001.
Values sent between devices are 32-bit elements; how exact they have to be, the bound alone decides.
A program may use at most 64 MiB of HBM per device.

v0:
```python
import jax
import jax.numpy as jnp
from jax import lax
from jax.sharding import PartitionSpec as P

SWEEPS = 6
CORRECTIONS = 2


step_fine = 1.0
step_coarse = 0.08


def extended_2(block, sides, width):
    for axis, dim in sides:
        count = lax.axis_size(axis)
        forward = [(i, i + 1) for i in range(count - 1)]
        backward = [(target, source) for source, target in forward]
        low = lax.ppermute(
            lax.slice_in_dim(block, block.shape[dim] - width, None, axis=dim), axis, forward
        )
        high = lax.ppermute(lax.slice_in_dim(block, 0, width, axis=dim), axis, backward)
        block = jnp.concatenate([low, block, high], axis=dim)
    return block


def neighbours(extended):
    core = extended[1:-1]
    total = extended[2:] + extended[:-2]
    wide = jnp.pad(core, ((0, 0), (1, 1), (0, 0)))
    total = total + wide[:, 2:] + wide[:, :-2]
    deeper = jnp.pad(core, ((0, 0), (0, 0), (1, 1)))
    return total + deeper[:, :, 2:] + deeper[:, :, :-2]


def jacobi_sweep(extended, previous, capacity, forcing, divisor):
    return (capacity * previous + step_fine * forcing + step_fine * neighbours(extended)) / divisor


def coarse_value_of(state, scale, forcing):
    extended = extended_2(state, (("space", 0),), 1)
    core = extended[1:-1]
    return core + scale * (neighbours(extended) - 6.0 * core + forcing)


def forcing_from(source, segment_index, control_row):
    matches = segment_index[:, None, :] == lax.broadcasted_iota(
        jnp.int32, (1, control_row.shape[0], 1), 1
    )
    values = jnp.sum(
        jnp.where(matches, control_row[None, :, None], jnp.zeros((), jnp.float32)), axis=1
    )
    return source + jnp.pad(values[:, None, :], ((0, 0), (0, source.shape[1] - 1), (0, 0)))


def on_device(initial_state, capacity, source, control, segment_index):
    forcing = forcing_from(source, segment_index, control[0])
    divisor = capacity + 6.0 * step_fine
    scale = step_coarse / capacity
    my_slice = lax.axis_index("tm")
    time_groups = lax.axis_size("tm")
    all_rows = lax.all_gather(control, "tm", axis=0, tiled=True)

    def run_chain(correction_term, first_chain):
        if first_chain:
            every_term = None
        else:
            every_term = lax.all_gather(correction_term[None], "tm", axis=0, tiled=True)

        def chain_section(section_index, state):
            row = lax.dynamic_index_in_dim(all_rows, section_index, 0, keepdims=False)
            section_forcing = forcing_from(source, segment_index, row)
            following = coarse_value_of(state, scale, section_forcing)
            if every_term is not None:
                following = following + lax.dynamic_index_in_dim(
                    every_term, section_index, 0, keepdims=False
                )
            return jnp.where(section_index < my_slice, following, state)

        start_state = lax.fori_loop(0, time_groups - 1, chain_section, initial_state)
        coarse_value = coarse_value_of(start_state, scale, forcing)
        return (start_state, coarse_value, coarse_value + correction_term)

    start_state, coarse_value, end_state = run_chain(jnp.zeros_like(initial_state), True)
    for correction_index in range(CORRECTIONS):
        fine_state = start_state
        iterate = fine_state
        for sweep_index in range(SWEEPS):
            extended = extended_2(iterate, (("space", 0),), 1)
            iterate = jacobi_sweep(extended, fine_state, capacity, forcing, divisor)
        fine_state = iterate
        correction_term = fine_state - coarse_value
        start_state, coarse_value, end_state = run_chain(correction_term, False)
    return end_state[None]


def solution(mesh):
    in_specs = (
        P("space", None, None),
        P("space", None, None),
        P("space", None, None),
        P("tm", None),
        P("space", None),
    )
    out_specs = P("tm", "space", None, None)
    return jax.shard_map(
        on_device, mesh=mesh, in_specs=in_specs, out_specs=out_specs, check_vma=False
    )
```

profile of v0, /device:TPU:23, one launch (start us, length us, event | category | flops | bytes accessed | tf_op | source)
XLA Modules:
  0.0 402.3 jit_solution(10666983679543721038)
XLA Ops:
  6.5 5.1 %all-gather.2 = f32[4,1,16]{2,1,0:T(1,128)S(1)} all-gather(f32[1,1,16]{2,1,0:T(1,128)} %bitcast.55), channel_id=1, replica_groups=mesh['tm'=4,'space'=8] {'tm'}, dimensions={0}, use_global_device_ids=true | all-gather | bytes 320 | tf_op jit(solution)/shard_map/all_gather | solution.py:62
  15.3 47.1 %while.45 = (s32[]{:T(128)}, f32[2,256,256]{2,0,1:T(2,128)S(1)}, s32[]{:T(128)}, s32[2,256]{1,0:T(2,128)S(1)}, f32[4,16]{1,0:T(4,128)S(1)}, /*index=5*/f32[2,256...) while((s32[]{:T(128)}, f32[2,256,256]{2,0,1:T(2,128)S(1)}, s32[]{:T(128)}, s32[2,256]{1,0:T(2,128)S(1)}, ...), condition=%wide.region_2.3_spmd, body=%wide.region_0.0_spmd.sunk | while | flops 1859075 | bytes 7870871 | solution.py:80
  16.6 5.8 %collective-permute-start = (f32[1,256,256]{2,0,1:T(1,128)}, f32[1,256,256]{2,0,1:T(1,128)S(1)}, u32[]{:S(2)}, u32[]{:S(2)}) collective-permute-start(f32[1,256,256]{2,0,1:T(1,128)} %get-tuple-element.818), channel_id=1, source_target_pairs={{0,1},{1,2},{2,3},{3,4},{4,5},{5,6},{6,7},{8,9},{9,10},{10,11},{11... | collective-permute-start | bytes 786440 | tf_op jit(solution)/shard_map/while/body/eval_jaxpr/ppermute | solution.py:19
  26.0 4.1 %collective-permute-done.1 = f32[1,256,256]{2,0,1:T(1,128)S(1)} collective-permute-done((f32[1,256,256]{2,0,1:T(1,128)S(1)}, f32[1,256,256]{2,0,1:T(1,128)S(1)}, u32[]{:S(2)}, u32[]{:S(2)}) %collective-permute-start.1) | collective-permute-done | bytes 262176 | tf_op jit(solution)/shard_map/while/body/eval_jaxpr/ppermute | solution.py:22
  40.4 4.1 %collective-permute-done.1 = f32[1,256,256]{2,0,1:T(1,128)S(1)} collective-permute-done((f32[1,256,256]{2,0,1:T(1,128)S(1)}, f32[1,256,256]{2,0,1:T(1,128)S(1)}, u32[]{:S(2)}, u32[]{:S(2)}) %collective-permute-start.1) | collective-permute-done | bytes 262176 | tf_op jit(solution)/shard_map/while/body/eval_jaxpr/ppermute | solution.py:22
  54.8 4.1 %collective-permute-done.1 = f32[1,256,256]{2,0,1:T(1,128)S(1)} collective-permute-done((f32[1,256,256]{2,0,1:T(1,128)S(1)}, f32[1,256,256]{2,0,1:T(1,128)S(1)}, u32[]{:S(2)}, u32[]{:S(2)}) %collective-permute-start.1) | collective-permute-done | bytes 262176 | tf_op jit(solution)/shard_map/while/body/eval_jaxpr/ppermute | solution.py:22
  64.7 3.6 collective-permute-start.7
  71.7 3.9 add_divide_fusion.1
  139.2 35.7 %all-gather.6.cloned.1.call-done = f32[8,256,256]{2,1,0:T(8,128)} async-done(((f32[2,256,256]{2,1,0:T(8,128)}), f32[8,256,256]{2,1,0:T(8,128)}) %all-gather.6.cloned.1.call-update) | async-done | bytes 2097168 | tf_op jit(solution)/shard_map/all_gather | solution.py:68
  174.9 46.7 %while.46 = (s32[]{:T(128)}, f32[2,256,256]{2,0,1:T(2,128)S(1)}, s32[]{:T(128)}, s32[2,256]{1,0:T(2,128)S(1)}, f32[4,16]{1,0:T(4,128)S(1)}, /*index=5*/f32[2,256...) while((s32[]{:T(128)}, f32[2,256,256]{2,0,1:T(2,128)S(1)}, ...), condition=%wide.region_6.7_spmd, body=%wide.region_4.6_spmd.sunk | while | flops 1990147 | bytes 9443747 | solution.py:80
  176.2 3.8 collective-permute-start.2
  183.6 4.1 %collective-permute-done.3 = f32[1,256,256]{2,0,1:T(1,128)S(1)} collective-permute-done((f32[1,256,256]{2,0,1:T(1,128)S(1)}, f32[1,256,256]{2,0,1:T(1,128)S(1)}, u32[]{:S(2)}, u32[]{:S(2)}) %collective-permute-start.3) | collective-permute-done | bytes 262176 | tf_op jit(solution)/shard_map/while/body/eval_jaxpr/ppermute | solution.py:22
  198.6 4.1 %collective-permute-done.3 = f32[1,256,256]{2,0,1:T(1,128)S(1)} collective-permute-done((f32[1,256,256]{2,0,1:T(1,128)S(1)}, f32[1,256,256]{2,0,1:T(1,128)S(1)}, u32[]{:S(2)}, u32[]{:S(2)}) %collective-permute-start.3) | collective-permute-done | bytes 262176 | tf_op jit(solution)/shard_map/while/body/eval_jaxpr/ppermute | solution.py:22
  213.5 4.1 %collective-permute-done.3 = f32[1,256,256]{2,0,1:T(1,128)S(1)} collective-permute-done((f32[1,256,256]{2,0,1:T(1,128)S(1)}, f32[1,256,256]{2,0,1:T(1,128)S(1)}, u32[]{:S(2)}, u32[]{:S(2)}) %collective-permute-start.3) | collective-permute-done | bytes 262176 | tf_op jit(solution)/shard_map/while/body/eval_jaxpr/ppermute | solution.py:22
  223.9 3.6 collective-permute-start.19
  230.9 3.9 add_divide_fusion
  299.0 35.9 %all-gather.8.cloned.1.call-done = f32[8,256,256]{2,1,0:T(8,128)} async-done(((f32[2,256,256]{2,1,0:T(8,128)}), f32[8,256,256]{2,1,0:T(8,128)}) %all-gather.8.cloned.1.call-update) | async-done | bytes 2097168 | tf_op jit(solution)/shard_map/all_gather | solution.py:68
  334.9 46.8 %while.47 = (s32[]{:T(128)}, f32[2,256,256]{2,0,1:T(2,128)S(1)}, s32[]{:T(128)}, s32[2,256]{1,0:T(2,128)S(1)}, f32[4,16]{1,0:T(4,128)S(1)}, /*index=5*/f32[2,256...) while((s32[]{:T(128)}, f32[2,256,256]{2,0,1:T(2,128)S(1)}, ...), condition=%wide.region_9.10_spmd, body=%wide.region_7.9_spmd.sunk | while | flops 1990147 | bytes 9443747 | solution.py:80
  336.2 3.8 collective-permute-start.4
  343.6 4.1 %collective-permute-done.5 = f32[1,256,256]{2,0,1:T(1,128)S(1)} collective-permute-done((f32[1,256,256]{2,0,1:T(1,128)S(1)}, f32[1,256,256]{2,0,1:T(1,128)S(1)}, u32[]{:S(2)}, u32[]{:S(2)}) %collective-permute-start.5) | collective-permute-done | bytes 262176 | tf_op jit(solution)/shard_map/while/body/eval_jaxpr/ppermute | solution.py:22
  358.6 4.1 %collective-permute-done.5 = f32[1,256,256]{2,0,1:T(1,128)S(1)} collective-permute-done((f32[1,256,256]{2,0,1:T(1,128)S(1)}, f32[1,256,256]{2,0,1:T(1,128)S(1)}, u32[]{:S(2)}, u32[]{:S(2)}) %collective-permute-start.5) | collective-permute-done | bytes 262176 | tf_op jit(solution)/shard_map/while/body/eval_jaxpr/ppermute | solution.py:22
  373.6 4.1 %collective-permute-done.5 = f32[1,256,256]{2,0,1:T(1,128)S(1)} collective-permute-done((f32[1,256,256]{2,0,1:T(1,128)S(1)}, f32[1,256,256]{2,0,1:T(1,128)S(1)}, u32[]{:S(2)}, u32[]{:S(2)}) %collective-permute-start.5) | collective-permute-done | bytes 262176 | tf_op jit(solution)/shard_map/while/body/eval_jaxpr/ppermute | solution.py:22
  384.0 3.6 collective-permute-start.31
  391.0 3.6 add_bitcast_fusion
  (190 shorter events, 238.7 us)
Async XLA Ops:
  6.5 168.3 %all-gather.6.cloned.1.call-start = ((), (), s32[]{:S(2)}) async-start(), calls=%async_computation | async-start | bytes 2621440 | tf_op jit(solution)/shard_map/all_gather | solution.py:68
  16.6 9.4 %collective-permute-start = (f32[1,256,256]{2,0,1:T(1,128)}, f32[1,256,256]{2,0,1:T(1,128)S(1)}, u32[]{:S(2)}, u32[]{:S(2)}) collective-permute-start(f32[1,256,256]{2,0,1:T(1,128)} %get-tuple-element.818), channel_id=1, source_target_pairs={{0,1},{1,2},{2,3},{3,4},{4,5},{5,6},{6,7},{8,9},{9,10},{10,11},{11... | collective-permute-start | bytes 786440 | tf_op jit(solution)/shard_map/while/body/eval_jaxpr/ppermute | solution.py:19
  22.4 7.7 %collective-permute-start.1 = (f32[1,256,256]{2,0,1:T(1,128)S(1)}, f32[1,256,256]{2,0,1:T(1,128)S(1)}, u32[]{:S(2)}, u32[]{:S(2)}) collective-permute-start(f32[1,256,256]{2,0,1:T(1,128)S(1)} %get-tuple-element.819), channel_id=1, source_target_pairs={{1,0},{2,1},{3,2},{4,3},{5,4},{6,5},{7,6},{9,8},{10,9},{11,10},{12... | collective-permute-start | bytes 786440 | tf_op jit(solution)/shard_map/while/body/eval_jaxpr/ppermute | solution.py:22
  36.8 7.7 %collective-permute-start.1 = (f32[1,256,256]{2,0,1:T(1,128)S(1)}, f32[1,256,256]{2,0,1:T(1,128)S(1)}, u32[]{:S(2)}, u32[]{:S(2)}) collective-permute-start(f32[1,256,256]{2,0,1:T(1,128)S(1)} %get-tuple-element.819), channel_id=1, source_target_pairs={{1,0},{2,1},{3,2},{4,3},{5,4},{6,5},{7,6},{9,8},{10,9},{11,10},{12... | collective-permute-start | bytes 786440 | tf_op jit(solution)/shard_map/while/body/eval_jaxpr/ppermute | solution.py:22
  51.2 7.7 %collective-permute-start.1 = (f32[1,256,256]{2,0,1:T(1,128)S(1)}, f32[1,256,256]{2,0,1:T(1,128)S(1)}, u32[]{:S(2)}, u32[]{:S(2)}) collective-permute-start(f32[1,256,256]{2,0,1:T(1,128)S(1)} %get-tuple-element.819), channel_id=1, source_target_pairs={{1,0},{2,1},{3,2},{4,3},{5,4},{6,5},{7,6},{9,8},{10,9},{11,10},{12... | collective-permute-start | bytes 786440 | tf_op jit(solution)/shard_map/while/body/eval_jaxpr/ppermute | solution.py:22
  62.8 8.0 %collective-permute-start.6 = (f32[1,256,256]{2,0,1:T(1,128)S(1)}, f32[1,256,256]{2,0,1:T(1,128)S(1)}, u32[]{:S(2)}, u32[]{:S(2)}) collective-permute-start(f32[1,256,256]{2,0,1:T(1,128)S(1)} %get-tuple-element.685), channel_id=1, source_target_pairs={{1,0},{2,1},{3,2},{4,3},{5,4},{6,5},{7,6},{9,8},{10,9},{11,10},{12... | collective-permute-start | bytes 786440 | tf_op jit(solution)/shard_map/ppermute | solution.py:22
  76.0 8.7 %collective-permute-start.8 = (f32[1,256,256]{2,0,1:T(1,128)S(1)}, f32[1,256,256]{2,0,1:T(1,128)S(1)}, u32[]{:S(2)}, u32[]{:S(2)}) collective-permute-start(f32[1,256,256]{2,0,1:T(1,128)S(1)} %get-tuple-element.683), channel_id=1, source_target_pairs={{1,0},{2,1},{3,2},{4,3},{5,4},{6,5},{7,6},{9,8},{10,9},{11,10},{12... | collective-permute-start | bytes 786440 | tf_op jit(solution)/shard_map/ppermute | solution.py:22
  88.4 8.7 %collective-permute-start.10 = (f32[1,256,256]{2,0,1:T(1,128)S(1)}, f32[1,256,256]{2,0,1:T(1,128)S(1)}, u32[]{:S(2)}, u32[]{:S(2)}) collective-permute-start(f32[1,256,256]{2,0,1:T(1,128)S(1)} %get-tuple-element.681), channel_id=1, source_target_pairs={{1,0},{2,1},{3,2},{4,3},{5,4},{6,5},{7,6},{9,8},{10,9},{11,10},{12... | collective-permute-start | bytes 786440 | tf_op jit(solution)/shard_map/ppermute | solution.py:22
  100.7 8.7 %collective-permute-start.12 = (f32[1,256,256]{2,0,1:T(1,128)S(1)}, f32[1,256,256]{2,0,1:T(1,128)S(1)}, u32[]{:S(2)}, u32[]{:S(2)}) collective-permute-start(f32[1,256,256]{2,0,1:T(1,128)S(1)} %get-tuple-element.679), channel_id=1, source_target_pairs={{1,0},{2,1},{3,2},{4,3},{5,4},{6,5},{7,6},{9,8},{10,9},{11,10},{12... | collective-permute-start | bytes 786440 | tf_op jit(solution)/shard_map/ppermute | solution.py:22
  113.1 8.9 %collective-permute-start.14 = (f32[1,256,256]{2,0,1:T(1,128)S(1)}, f32[1,256,256]{2,0,1:T(1,128)S(1)}, u32[]{:S(2)}, u32[]{:S(2)}) collective-permute-start(f32[1,256,256]{2,0,1:T(1,128)S(1)} %get-tuple-element.677), channel_id=1, source_target_pairs={{1,0},{2,1},{3,2},{4,3},{5,4},{6,5},{7,6},{9,8},{10,9},{11,10},{12... | collective-permute-start | bytes 786440 | tf_op jit(solution)/shard_map/ppermute | solution.py:22
  125.6 8.7 %collective-permute-start.16 = (f32[1,256,256]{2,0,1:T(1,128)S(1)}, f32[1,256,256]{2,0,1:T(1,128)S(1)}, u32[]{:S(2)}, u32[]{:S(2)}) collective-permute-start(f32[1,256,256]{2,0,1:T(1,128)S(1)} %get-tuple-element.675), channel_id=1, source_target_pairs={{1,0},{2,1},{3,2},{4,3},{5,4},{6,5},{7,6},{9,8},{10,9},{11,10},{12... | collective-permute-start | bytes 786440 | tf_op jit(solution)/shard_map/ppermute | solution.py:22
  139.0 195.9 %all-gather.8.cloned.1.call-start = ((), (), s32[]{:S(2)}) async-start(), calls=%async_computation.1 | async-start | bytes 2621440 | tf_op jit(solution)/shard_map/all_gather | solution.py:68
  180.0 7.7 %collective-permute-start.3 = (f32[1,256,256]{2,0,1:T(1,128)S(1)}, f32[1,256,256]{2,0,1:T(1,128)S(1)}, u32[]{:S(2)}, u32[]{:S(2)}) collective-permute-start(f32[1,256,256]{2,0,1:T(1,128)S(1)} %get-tuple-element.829), channel_id=1, source_target_pairs={{1,0},{2,1},{3,2},{4,3},{5,4},{6,5},{7,6},{9,8},{10,9},{11,10},{12... | collective-permute-start | bytes 786440 | tf_op jit(solution)/shard_map/while/body/eval_jaxpr/ppermute | solution.py:22
  194.9 7.7 %collective-permute-start.3 = (f32[1,256,256]{2,0,1:T(1,128)S(1)}, f32[1,256,256]{2,0,1:T(1,128)S(1)}, u32[]{:S(2)}, u32[]{:S(2)}) collective-permute-start(f32[1,256,256]{2,0,1:T(1,128)S(1)} %get-tuple-element.829), channel_id=1, source_target_pairs={{1,0},{2,1},{3,2},{4,3},{5,4},{6,5},{7,6},{9,8},{10,9},{11,10},{12... | collective-permute-start | bytes 786440 | tf_op jit(solution)/shard_map/while/body/eval_jaxpr/ppermute | solution.py:22
  209.9 7.7 %collective-permute-start.3 = (f32[1,256,256]{2,0,1:T(1,128)S(1)}, f32[1,256,256]{2,0,1:T(1,128)S(1)}, u32[]{:S(2)}, u32[]{:S(2)}) collective-permute-start(f32[1,256,256]{2,0,1:T(1,128)S(1)} %get-tuple-element.829), channel_id=1, source_target_pairs={{1,0},{2,1},{3,2},{4,3},{5,4},{6,5},{7,6},{9,8},{10,9},{11,10},{12... | collective-permute-start | bytes 786440 | tf_op jit(solution)/shard_map/while/body/eval_jaxpr/ppermute | solution.py:22
  222.0 8.0 %collective-permute-start.18 = (f32[1,256,256]{2,0,1:T(1,128)S(1)}, f32[1,256,256]{2,0,1:T(1,128)S(1)}, u32[]{:S(2)}, u32[]{:S(2)}) collective-permute-start(f32[1,256,256]{2,0,1:T(1,128)S(1)} %get-tuple-element.673), channel_id=1, source_target_pairs={{1,0},{2,1},{3,2},{4,3},{5,4},{6,5},{7,6},{9,8},{10,9},{11,10},{12... | collective-permute-start | bytes 786440 | tf_op jit(solution)/shard_map/ppermute | solution.py:22
  235.2 8.7 %collective-permute-start.20 = (f32[1,256,256]{2,0,1:T(1,128)S(1)}, f32[1,256,256]{2,0,1:T(1,128)S(1)}, u32[]{:S(2)}, u32[]{:S(2)}) collective-permute-start(f32[1,256,256]{2,0,1:T(1,128)S(1)} %get-tuple-element.671), channel_id=1, source_target_pairs={{1,0},{2,1},{3,2},{4,3},{5,4},{6,5},{7,6},{9,8},{10,9},{11,10},{12... | collective-permute-start | bytes 786440 | tf_op jit(solution)/shard_map/ppermute | solution.py:22
  247.6 8.7 %collective-permute-start.22 = (f32[1,256,256]{2,0,1:T(1,128)S(1)}, f32[1,256,256]{2,0,1:T(1,128)S(1)}, u32[]{:S(2)}, u32[]{:S(2)}) collective-permute-start(f32[1,256,256]{2,0,1:T(1,128)S(1)} %get-tuple-element.669), channel_id=1, source_target_pairs={{1,0},{2,1},{3,2},{4,3},{5,4},{6,5},{7,6},{9,8},{10,9},{11,10},{12... | collective-permute-start | bytes 786440 | tf_op jit(solution)/shard_map/ppermute | solution.py:22
  260.0 8.7 %collective-permute-start.24 = (f32[1,256,256]{2,0,1:T(1,128)S(1)}, f32[1,256,256]{2,0,1:T(1,128)S(1)}, u32[]{:S(2)}, u32[]{:S(2)}) collective-permute-start(f32[1,256,256]{2,0,1:T(1,128)S(1)} %get-tuple-element.667), channel_id=1, source_target_pairs={{1,0},{2,1},{3,2},{4,3},{5,4},{6,5},{7,6},{9,8},{10,9},{11,10},{12... | collective-permute-start | bytes 786440 | tf_op jit(solution)/shard_map/ppermute | solution.py:22
  272.3 8.9 %collective-permute-start.26 = (f32[1,256,256]{2,0,1:T(1,128)S(1)}, f32[1,256,256]{2,0,1:T(1,128)S(1)}, u32[]{:S(2)}, u32[]{:S(2)}) collective-permute-start(f32[1,256,256]{2,0,1:T(1,128)S(1)} %get-tuple-element.665), channel_id=1, source_target_pairs={{1,0},{2,1},{3,2},{4,3},{5,4},{6,5},{7,6},{9,8},{10,9},{11,10},{12... | collective-permute-start | bytes 786440 | tf_op jit(solution)/shard_map/ppermute | solution.py:22
  284.8 8.7 %collective-permute-start.28 = (f32[1,256,256]{2,0,1:T(1,128)S(1)}, f32[1,256,256]{2,0,1:T(1,128)S(1)}, u32[]{:S(2)}, u32[]{:S(2)}) collective-permute-start(f32[1,256,256]{2,0,1:T(1,128)S(1)} %get-tuple-element.663), channel_id=1, source_target_pairs={{1,0},{2,1},{3,2},{4,3},{5,4},{6,5},{7,6},{9,8},{10,9},{11,10},{12... | collective-permute-start | bytes 786440 | tf_op jit(solution)/shard_map/ppermute | solution.py:22
  340.0 7.7 %collective-permute-start.5 = (f32[1,256,256]{2,0,1:T(1,128)S(1)}, f32[1,256,256]{2,0,1:T(1,128)S(1)}, u32[]{:S(2)}, u32[]{:S(2)}) collective-permute-start(f32[1,256,256]{2,0,1:T(1,128)S(1)} %get-tuple-element.839), channel_id=1, source_target_pairs={{1,0},{2,1},{3,2},{4,3},{5,4},{6,5},{7,6},{9,8},{10,9},{11,10},{12... | collective-permute-start | bytes 786440 | tf_op jit(solution)/shard_map/while/body/eval_jaxpr/ppermute | solution.py:22
  355.0 7.7 %collective-permute-start.5 = (f32[1,256,256]{2,0,1:T(1,128)S(1)}, f32[1,256,256]{2,0,1:T(1,128)S(1)}, u32[]{:S(2)}, u32[]{:S(2)}) collective-permute-start(f32[1,256,256]{2,0,1:T(1,128)S(1)} %get-tuple-element.839), channel_id=1, source_target_pairs={{1,0},{2,1},{3,2},{4,3},{5,4},{6,5},{7,6},{9,8},{10,9},{11,10},{12... | collective-permute-start | bytes 786440 | tf_op jit(solution)/shard_map/while/body/eval_jaxpr/ppermute | solution.py:22
  382.1 8.0 %collective-permute-start.30 = (f32[1,256,256]{2,0,1:T(1,128)S(1)}, f32[1,256,256]{2,0,1:T(1,128)S(1)}, u32[]{:S(2)}, u32[]{:S(2)}) collective-permute-start(f32[1,256,256]{2,0,1:T(1,128)S(1)} %get-tuple-element.661), channel_id=1, source_target_pairs={{1,0},{2,1},{3,2},{4,3},{5,4},{6,5},{7,6},{9,8},{10,9},{11,10},{12... | collective-permute-start | bytes 786440 | tf_op jit(solution)/shard_map/ppermute | solution.py:22
  (37 other events, 256.3 us)
Sparse Core Ops, SparseCore 0:
  139.1 35.7 all-gather.5
  299.1 35.7 all-gather.7
where the time goes:
time: 406 us; the launch traced here: 402 us
  waiting for transfers between devices  155 us (38%)
  starting transfers between devices  126 us (31%)
  other arithmetic  65.4 us (16%)
  local copies, waits for them, and re-layouts  36.4 us (9%)
  between operations  13.9 us (3%)
  blocking collectives  5.06 us (1%)
    all_gather x2, waiting for transfers between devices, run_chain(): every_term = lax.all_gather(correction_term[None], 'tm', axis=0, tiled=True)  71.5 us
    ppermute x22, waiting for transfers between devices, extended_2(): lax.ppermute(lax.slice_in_dim(block, 0, width, axis=dim), axis, backward)  67.5 us
    ppermute x22, starting transfers between devices, extended_2(): lax.ppermute(lax.slice_in_dim(block, block.shape[dim] - width, None, axis...  66.8 us
    ppermute x22, starting transfers between devices, extended_2(): lax.ppermute(lax.slice_in_dim(block, 0, width, axis=dim), axis, backward)  58.8 us
    select_n x9, other arithmetic, chain_section(): return jnp.where(section_index < my_slice, following, state)  28.2 us
    div x10, other arithmetic, jacobi_sweep(): (capacity * previous + step_fine * forcing + step_fine * neighbours(exten...  26.4 us
    ppermute x22, waiting for transfers between devices, extended_2(): lax.ppermute(lax.slice_in_dim(block, block.shape[dim] - width, None, axis...  16.3 us
    slice x22, local copies, waits for them, and re-layouts, extended_2(): lax.slice_in_dim(block, 0, width, axis=dim)  15.3 us
  transfers between devices with their start and end apart: 46, of which 42 were waited for; matrix products, arithmetic and copies ran while one was open for 2% of the time, Pallas kernels for 0%

commit v1 on v0

v1 whole, which is shorter than its diff:
```python
import functools

import jax
import jax.numpy as jnp
from jax import lax
from jax.experimental import pallas as pl
from jax.experimental.pallas import tpu as pltpu
from jax.sharding import PartitionSpec as P

SWEEPS = 6
CORRECTIONS = 2
step_fine = 1.0
step_coarse = 0.08


def make_plan(slices):
    last = CORRECTIONS
    solves = [
        (k, n)
        for k in range(last)
        for n in range(k, slices)
        if k == last - 1 or n + 1 < slices or n == k
    ]
    slots, sent = {}, set()
    for k, n in solves:
        for j in range(SWEEPS):
            slots[(k, n, j)] = len(slots)
            sent.add((k, n, j))

    def state(k, n):
        k = min(k, n)
        key = (k, n, 0)
        if key not in slots:
            slots[key] = len(slots)
        return key

    ends = [state(last, n + 1) for n in range(slices)]
    rounds = {}
    top_coarse = max(n for k, n in solves if k == 0)
    for n in range(top_coarse):
        rounds.setdefault(n + 1, []).append(("coarse", n, state(0, n), state(0, n + 1)))
    for k, n in sorted(solves, key=lambda item: (-item[0], item[1])):
        begin = SWEEPS * k + n - k
        for j in range(1, SWEEPS + 1):
            target = (k, n, j) if j < SWEEPS else state(k + 1, n + 1)
            pair = None
            if j == SWEEPS and k < n:
                pair = (state(k + 1, n), state(k, n))
                sent.add(pair[0])
                sent.add(pair[1])
            rounds.setdefault(begin + j, []).append(("sweep", n, (k, n, j - 1), target, j, pair))
    return slots, sent, [rounds[r] for r in sorted(rounds)], ends


def kernel(plan, size, state_hbm, cap_hbm, src_hbm, ctrl_ref, seg_ref, out_hbm,
           field, forcing, base, inv, scale, source, ctrl_all,
           send_sem, recv_sem, in_sem, ctrl_send, ctrl_recv, out_send, out_recv, own_sem):
    slots, sent, rounds, ends = plan
    planes, window, own_rows, reach, rows, cols, slices, count = size
    t = lax.axis_index("tm")
    s = lax.axis_index("space")
    low_there, high_there = s > 0, s < count - 1
    first_row = pl.multiple_of(jnp.clip(t * own_rows - reach, 0, rows - window), 8)
    own_at = pl.multiple_of(t * own_rows - first_row, 8)
    inner = pl.ds(1, planes)
    first = slots[(0, 0, 0)]

    loads = []
    for index, (ref, target) in enumerate(
        ((state_hbm, field.at[first, inner]), (cap_hbm, inv), (src_hbm, source))
    ):
        loads.append(pltpu.make_async_copy(ref.at[:, pl.ds(first_row, window), :], target, in_sem.at[index]))
        loads[-1].start()

    @pl.when(jnp.logical_not(low_there))
    def _():
        for key in sorted(sent):
            field[slots[key], 0] = jnp.zeros((window, cols), jnp.float32)

    @pl.when(jnp.logical_not(high_there))
    def _():
        for key in sorted(sent):
            field[slots[key], planes + 1] = jnp.zeros((window, cols), jnp.float32)

    barrier = pltpu.get_barrier_semaphore()

    @pl.when(low_there)
    def _():
        pl.semaphore_signal(barrier, inc=1, device_id={"space": s - 1})

    @pl.when(high_there)
    def _():
        pl.semaphore_signal(barrier, inc=1, device_id={"space": s + 1})

    for hop in range(1, slices):
        pl.semaphore_signal(barrier, inc=1, device_id={"tm": lax.rem(t + hop, slices)})
    pl.semaphore_wait(barrier, slices - 1 + jnp.minimum(s, 1) + jnp.minimum(count - 1 - s, 1))

    def halo(key, side):
        slot = slots[key]
        if side == 0:
            source_plane, target_plane, other = 1, planes + 1, s - 1
        else:
            source_plane, target_plane, other = planes, 0, s + 1
        return pltpu.make_async_remote_copy(
            src_ref=field.at[slot, source_plane],
            dst_ref=field.at[slot, target_plane],
            send_sem=send_sem.at[slot, side],
            recv_sem=recv_sem.at[slot, side],
            device_id={"space": other},
        )

    def send(key):
        if key in sent:
            for side, there in ((0, low_there), (1, high_there)):

                @pl.when(there)
                def _():
                    halo(key, side).start()

    arrived = set()

    def arrive(key):
        if key in arrived:
            return
        arrived.add(key)
        for side, there in ((0, high_there), (1, low_there)):

            @pl.when(there)
            def _():
                halo(key, side).wait_recv()

    loads[0].wait()
    send((0, 0, 0))

    ctrl_copies = []
    for hop in range(1, slices):
        ctrl_copies.append(pltpu.make_async_remote_copy(
            src_ref=ctrl_ref,
            dst_ref=ctrl_all.at[hop],
            send_sem=ctrl_send.at[hop],
            recv_sem=ctrl_recv.at[hop],
            device_id={"tm": lax.rem(t + hop, slices)},
        ))
        ctrl_copies[-1].start()
    own_ctrl = pltpu.make_async_copy(ctrl_ref, ctrl_all.at[0], own_sem.at[0])
    own_ctrl.start()

    loads[1].wait()
    capacity = inv[...]
    scale[...] = step_coarse / capacity
    reciprocal = 1.0 / (capacity + 6.0 * step_fine)
    inv[...] = reciprocal
    loads[2].wait()
    own_ctrl.wait()
    for copy in ctrl_copies:
        copy.wait_recv()

    segment = seg_ref[...]
    segments = ctrl_ref.shape[1]
    row_id = lax.broadcasted_iota(jnp.int32, (planes, window, cols), 1) + first_row
    for n in range(slices):
        row = jnp.zeros((1, segments), jnp.float32)
        for hop in range(slices):
            row = jnp.where(lax.rem(t - n + slices, slices) == hop, ctrl_all[hop], row)
        values = jnp.zeros((planes, cols), jnp.float32)
        for k in range(segments):
            values = jnp.where(segment == k, row[:, k:k + 1], values)
        forcing[n] = source[...] + jnp.where(row_id == 0, values[:, None, :], 0.0)

    step = window // 2 if window % 16 == 0 else window
    lane = lax.broadcasted_iota(jnp.int32, (step, cols), 1)
    line = lax.broadcasted_iota(jnp.int32, (step, cols), 0)
    pieces = [(p, r) for p in range(planes) for r in range(0, window, step)]

    def neighbours(read, p, r):
        core = read(p + 1, r)
        if r > 0:
            above = read(p + 1, r - 1)
        else:
            above = jnp.where(line == 0, 0.0, pltpu.roll(core, 1, 0))
        if r + step < window:
            below = read(p + 1, r + 1)
        else:
            below = jnp.where(line == step - 1, 0.0, pltpu.roll(core, step - 1, 0))
        left = jnp.where(lane == 0, 0.0, pltpu.roll(core, 1, 1))
        right = jnp.where(lane == cols - 1, 0.0, pltpu.roll(core, cols - 1, 1))
        return core, read(p, r) + read(p + 2, r) + above + below + left + right

    def reader(key):
        return lambda p, r: field[slots[key], p, pl.ds(r, step)]

    def difference(new, old):
        return lambda p, r: field[slots[new], p, pl.ds(r, step)] - field[slots[old], p, pl.ds(r, step)]

    def piece(ref, p, r):
        return ref[p, pl.ds(r, step)]

    def result(n, end):
        def remote(target, source_slice):
            return pltpu.make_async_remote_copy(
                src_ref=field.at[slots[end], inner, pl.ds(own_at, own_rows)],
                dst_ref=out_hbm.at[0, :, pl.ds(pl.multiple_of(source_slice * own_rows, 8), own_rows)],
                send_sem=out_send.at[target],
                recv_sem=out_recv.at[source_slice],
                device_id={"tm": target},
            )
        return remote

    def own_copy(n):
        return pltpu.make_async_copy(
            field.at[slots[ends[n]], inner, pl.ds(own_at, own_rows)],
            out_hbm.at[0, :, pl.ds(n * own_rows, own_rows)],
            own_sem.at[1],
        )

    def emit(key):
        for n, end in enumerate(ends):
            if end == key:

                @pl.when(t != n)
                def _():
                    result(n, end)(n, t).start()

                @pl.when(t == n)
                def _():
                    own_copy(n).start()

    for tasks in rounds:
        for task in tasks:
            if task[0] == "coarse":
                _, n, source_key, target = task
                arrive(source_key)
                for p, r in pieces:
                    core, around = neighbours(reader(source_key), p, r)
                    field[slots[target], p + 1, pl.ds(r, step)] = core + piece(scale, p, r) * (
                        around - 6.0 * core + piece(forcing.at[n], p, r)
                    )
            else:
                _, n, source_key, target, j, pair = task
                held = source_key[0] % 2 * slices + n
                arrive(source_key)
                if pair is not None:
                    arrive(pair[0])
                    arrive(pair[1])
                for p, r in pieces:
                    core, around = neighbours(reader(source_key), p, r)
                    gain = piece(inv, p, r)
                    if j == 1:
                        constant = core - gain * (6.0 * step_fine * core - step_fine * piece(forcing.at[n], p, r))
                        base[held, p, pl.ds(r, step)] = constant
                    else:
                        constant = piece(base.at[held], p, r)
                    value = constant + step_fine * gain * around
                    if pair is not None:
                        change, spread = neighbours(difference(*pair), p, r)
                        value = value + change + piece(scale, p, r) * (spread - 6.0 * change)
                    field[slots[target], p + 1, pl.ds(r, step)] = value
            send(target)
            emit(target)

    for key in sorted(sent):
        arrive(key)
        for side, there in ((0, low_there), (1, high_there)):

            @pl.when(there)
            def _():
                halo(key, side).wait_send()

    for copy in ctrl_copies:
        copy.wait_send()
    for n in range(slices):

        @pl.when(t != n)
        def _():
            result(n, ends[n])(n, t).wait_send()
            result(n, ends[n])(t, n).wait_recv()

        @pl.when(t == n)
        def _():
            own_copy(n).wait()


def solution(mesh):
    slices, count = mesh.shape["tm"], mesh.shape["space"]
    plan = make_plan(slices)

    def on_device(initial_state, capacity, source, control, segment_index):
        planes, rows, cols = initial_state.shape
        own_rows = rows // slices
        reach = -(-(CORRECTIONS * SWEEPS + slices - CORRECTIONS) // 8) * 8
        window = min(rows, own_rows + 2 * reach)
        fields = len(plan[0])
        size = (planes, window, own_rows, reach, rows, cols, slices, count)
        block = (planes, window, cols)
        dma = pltpu.SemaphoreType.DMA
        return pl.pallas_call(
            functools.partial(kernel, plan, size),
            out_shape=jax.ShapeDtypeStruct((1, planes, rows, cols), jnp.float32),
            in_specs=[pl.BlockSpec(memory_space=pl.ANY)] * 3 + [pl.BlockSpec(memory_space=pltpu.VMEM)] * 2,
            out_specs=pl.BlockSpec(memory_space=pl.ANY),
            scratch_shapes=[
                pltpu.VMEM((fields, planes + 2, window, cols), jnp.float32),
                pltpu.VMEM((slices,) + block, jnp.float32),
                pltpu.VMEM((2 * slices,) + block, jnp.float32),
                pltpu.VMEM(block, jnp.float32),
                pltpu.VMEM(block, jnp.float32),
                pltpu.VMEM(block, jnp.float32),
                pltpu.VMEM((slices,) + control.shape, jnp.float32),
                dma((fields, 2)),
                dma((fields, 2)),
                dma((3,)),
                dma((slices,)),
                dma((slices,)),
                dma((slices,)),
                dma((slices,)),
                dma((2,)),
            ],
            compiler_params=pltpu.CompilerParams(
                collective_id=0, has_side_effects=True, vmem_limit_bytes=67043328 - 1048576
            ),
        )(initial_state, capacity, source, control, segment_index)

    return jax.shard_map(
        on_device,
        mesh=mesh,
        in_specs=(
            P("space", None, None),
            P("space", None, None),
            P("space", None, None),
            P("tm", None),
            P("space", None),
        ),
        out_specs=P("tm", "space", None, None),
        check_vma=False,
    )
```

time: 406 us -> 66 us (0.16)
  waiting for transfers between devices: 155 us -> 0 us
  starting transfers between devices: 126 us -> 0 us
  other arithmetic: 65.4 us -> 0 us
  Pallas kernels: 0 us -> 63.9 us
  local copies, waits for them, and re-layouts: 36.4 us -> 1.87 us
  between operations: 13.9 us -> 0.01 us
  blocking collectives: 5.06 us -> 0 us
    ppermute x44 -> x0, starting transfers between devices: 126 us -> none  [the longest x22 66.8 us: extended_2(): lax.ppermute(lax.slice_in_dim(block, block.shape[dim] - width, None, axis...]
    ppermute x44 -> x0, waiting for transfers between devices: 83.8 us -> none  [the longest x22 67.5 us: extended_2(): lax.ppermute(lax.slice_in_dim(block, 0, width, axis=dim), axis, backward)]
    all_gather x2 -> x0, waiting for transfers between devices: 71.5 us -> none  [run_chain(): every_term = lax.all_gather(correction_term[None], 'tm', axis=0, tiled=True)]
    pallas_call x0 -> x1, Pallas kernels: none -> 63.9 us  [on_device(): pl.pallas_call(functools.partial(kernel, plan, size), out_shape=jax.Shape...]
    select_n x9 -> x0, other arithmetic: 28.2 us -> none  [chain_section(): return jnp.where(section_index < my_slice, following, state)]
    div x11 -> x0, other arithmetic: 26.9 us -> none  [the longest x10 26.4 us: jacobi_sweep(): (capacity * previous + step_fine * forcing + step_fine * neighbours(exten...]
    slice x22 -> x0, local copies, waits for them, and re-layouts: 15.3 us -> none  [extended_2(): lax.slice_in_dim(block, 0, width, axis=dim)]
    while x29 -> x0, local copies, waits for them, and re-layouts: 10.9 us -> none
  transfers between devices with their start and end apart: 46 -> 0, of which waited for: 42 -> 0; matrix products, arithmetic and copies ran while one was open for 2% -> 0% of each run, Pallas kernels for 0% -> 0%
where the time goes in v1:
time: 66 us; the launch traced here: 65.8 us
  Pallas kernels  63.9 us (97%)
  local copies, waits for them, and re-layouts  1.87 us (3%)
    pallas_call x1, Pallas kernels, on_device(): pl.pallas_call(functools.partial(kernel, plan, size), out_shape=jax.Shape...  63.9 us
    unnamed x1, local copies, waits for them, and re-layouts  1.87 us

profile of v1, /device:TPU:23, one launch (start us, length us, event | category | flops | bytes accessed | tf_op | source)
XLA Modules:
  0.0 65.8 jit_solution(10768450622725000312)
XLA Ops:
  0.0 63.9 %shard_map.55 = f32[1,2,256,256]{3,2,1,0:T(8,128)} custom-call(f32[2,256,256]{2,1,0:T(8,128)} %state_hbm.1, f32[2,256,256]{2,1,0:T(8,128)} %cap_hbm.1, f32[2,256,256]{2,1,0:T(8,128)} %src_hbm.1, f32[1,16]{1,0:T(1,128)} %ctrl_ref.1, s32[2,256]{1,0:T(2,128)} %seg_ref.1), custom_call_target="tpu_custom_call" | custom-call | tf_op jit(solution)/shard_map/pallas_call | solution.py:297
  63.9 1.9 %copy.7 = f32[1,2,256,256]{3,2,1,0:T(8,128)} copy(f32[1,2,256,256]{3,2,1,0:T(8,128)} %shard_map.55) | data formatting | bytes 1048576

commit v2 on v1

--- a/solution.py
+++ b/solution.py
@@ -52,16 +52,29 @@
     return slots, sent, [rounds[r] for r in sorted(rounds)], ends
 
 
+def row_order(groups):
+    if groups & (groups - 1):
+        return list(range(groups))
+    return [i ^ (i >> 1) for i in range(groups)]
+
+
 def kernel(plan, size, state_hbm, cap_hbm, src_hbm, ctrl_ref, seg_ref, out_hbm,
-           field, forcing, base, inv, scale, source, ctrl_all,
-           send_sem, recv_sem, in_sem, ctrl_send, ctrl_recv, out_send, out_recv, own_sem):
+           field, edge, forcing, base, inv, scale, source, ctrl_all,
+           send_sem, recv_sem, in_sem, ctrl_send, ctrl_recv, out_send, out_recv, own_sem,
+           edge_send, edge_recv):
     slots, sent, rounds, ends = plan
-    planes, window, own_rows, reach, rows, cols, slices, count = size
+    planes, own_rows, rows, cols, slices, count = size
     t = lax.axis_index("tm")
     s = lax.axis_index("space")
     low_there, high_there = s > 0, s < count - 1
-    first_row = pl.multiple_of(jnp.clip(t * own_rows - reach, 0, rows - window), 8)
-    own_at = pl.multiple_of(t * own_rows - first_row, 8)
+    order = row_order(slices)
+    block, before, after = 0, 0, 0
+    for place, group in enumerate(order):
+        block = jnp.where(t == group, place, block)
+        before = jnp.where(t == group, order[max(place - 1, 0)], before)
+        after = jnp.where(t == group, order[min(place + 1, slices - 1)], after)
+    before_there, after_there = block > 0, block < slices - 1
+    first_row = pl.multiple_of(block * own_rows, 8)
     inner = pl.ds(1, planes)
     first = slots[(0, 0, 0)]
 
@@ -69,18 +82,25 @@
     for index, (ref, target) in enumerate(
         ((state_hbm, field.at[first, inner]), (cap_hbm, inv), (src_hbm, source))
     ):
-        loads.append(pltpu.make_async_copy(ref.at[:, pl.ds(first_row, window), :], target, in_sem.at[index]))
+        loads.append(pltpu.make_async_copy(ref.at[:, pl.ds(first_row, own_rows), :], target, in_sem.at[index]))
         loads[-1].start()
 
     @pl.when(jnp.logical_not(low_there))
     def _():
         for key in sorted(sent):
-            field[slots[key], 0] = jnp.zeros((window, cols), jnp.float32)
+            field[slots[key], 0] = jnp.zeros((own_rows, cols), jnp.float32)
 
     @pl.when(jnp.logical_not(high_there))
     def _():
         for key in sorted(sent):
-            field[slots[key], planes + 1] = jnp.zeros((window, cols), jnp.float32)
+            field[slots[key], planes + 1] = jnp.zeros((own_rows, cols), jnp.float32)
+
+    for side, there in ((0, before_there), (1, after_there)):
+
+        @pl.when(jnp.logical_not(there))
+        def _():
+            for key in sorted(sent):
+                edge[slots[key], side] = jnp.zeros((planes, 8, cols), jnp.float32)
 
     barrier = pltpu.get_barrier_semaphore()
 
@@ -110,6 +130,16 @@
             device_id={"space": other},
         )
 
+    def rim(key, side):
+        slot = slots[key]
+        return pltpu.make_async_remote_copy(
+            src_ref=field.at[slot, inner, pl.ds(0 if side == 0 else own_rows - 8, 8)],
+            dst_ref=edge.at[slot, 1 - side],
+            send_sem=edge_send.at[slot, side],
+            recv_sem=edge_recv.at[slot, side],
+            device_id={"tm": before if side == 0 else after},
+        )
+
     def send(key):
         if key in sent:
             for side, there in ((0, low_there), (1, high_there)):
@@ -117,6 +147,12 @@
                 @pl.when(there)
                 def _():
                     halo(key, side).start()
+
+            for side, there in ((0, before_there), (1, after_there)):
+
+                @pl.when(there)
+                def _():
+                    rim(key, side).start()
 
     arrived = set()
 
@@ -129,6 +165,12 @@
             @pl.when(there)
             def _():
                 halo(key, side).wait_recv()
+
+        for side, there in ((0, after_there), (1, before_there)):
+
+            @pl.when(there)
+            def _():
+                rim(key, side).wait_recv()
 
     loads[0].wait()
     send((0, 0, 0))
@@ -158,7 +200,7 @@
 
     segment = seg_ref[...]
     segments = ctrl_ref.shape[1]
-    row_id = lax.broadcasted_iota(jnp.int32, (planes, window, cols), 1) + first_row
+    row_id = lax.broadcasted_iota(jnp.int32, (planes, own_rows, cols), 1) + first_row
     for n in range(slices):
         row = jnp.zeros((1, segments), jnp.float32)
         for hop in range(slices):
@@ -168,30 +210,37 @@
             values = jnp.where(segment == k, row[:, k:k + 1], values)
         forcing[n] = source[...] + jnp.where(row_id == 0, values[:, None, :], 0.0)
 
-    step = window // 2 if window % 16 == 0 else window
+    step = own_rows // 2 if own_rows % 16 == 0 else own_rows
     lane = lax.broadcasted_iota(jnp.int32, (step, cols), 1)
     line = lax.broadcasted_iota(jnp.int32, (step, cols), 0)
-    pieces = [(p, r) for p in range(planes) for r in range(0, window, step)]
+    pieces = [(p, r) for p in range(planes) for r in range(0, own_rows, step)]
 
     def neighbours(read, p, r):
         core = read(p + 1, r)
         if r > 0:
             above = read(p + 1, r - 1)
         else:
-            above = jnp.where(line == 0, 0.0, pltpu.roll(core, 1, 0))
-        if r + step < window:
+            above = jnp.where(line == 0, read(p, None, 0), pltpu.roll(core, 1, 0))
+        if r + step < own_rows:
             below = read(p + 1, r + 1)
         else:
-            below = jnp.where(line == step - 1, 0.0, pltpu.roll(core, step - 1, 0))
+            below = jnp.where(line == step - 1, read(p, None, 1), pltpu.roll(core, step - 1, 0))
         left = jnp.where(lane == 0, 0.0, pltpu.roll(core, 1, 1))
         right = jnp.where(lane == cols - 1, 0.0, pltpu.roll(core, cols - 1, 1))
         return core, read(p, r) + read(p + 2, r) + above + below + left + right
 
     def reader(key):
-        return lambda p, r: field[slots[key], p, pl.ds(r, step)]
+        slot = slots[key]
+
+        def read(p, r, side=0):
+            if r is None:
+                return edge[slot, side, p, 7:8] if side == 0 else edge[slot, side, p, 0:1]
+            return field[slot, p, pl.ds(r, step)]
+
+        return read
 
     def difference(new, old):
-        return lambda p, r: field[slots[new], p, pl.ds(r, step)] - field[slots[old], p, pl.ds(r, step)]
+        return lambda *place: reader(new)(*place) - reader(old)(*place)
 
     def piece(ref, p, r):
         return ref[p, pl.ds(r, step)]
@@ -199,8 +248,8 @@
     def result(n, end):
         def remote(target, source_slice):
             return pltpu.make_async_remote_copy(
-                src_ref=field.at[slots[end], inner, pl.ds(own_at, own_rows)],
-                dst_ref=out_hbm.at[0, :, pl.ds(pl.multiple_of(source_slice * own_rows, 8), own_rows)],
+                src_ref=field.at[slots[end], inner],
+                dst_ref=out_hbm.at[0, :, pl.ds(first_row, own_rows)],
                 send_sem=out_send.at[target],
                 recv_sem=out_recv.at[source_slice],
                 device_id={"tm": target},
@@ -209,8 +258,8 @@
 
     def own_copy(n):
         return pltpu.make_async_copy(
-            field.at[slots[ends[n]], inner, pl.ds(own_at, own_rows)],
-            out_hbm.at[0, :, pl.ds(n * own_rows, own_rows)],
+            field.at[slots[ends[n]], inner],
+            out_hbm.at[0, :, pl.ds(first_row, own_rows)],
             own_sem.at[1],
         )
 
@@ -267,6 +316,12 @@
             def _():
                 halo(key, side).wait_send()
 
+        for side, there in ((0, before_there), (1, after_there)):
+
+            @pl.when(there)
+            def _():
+                rim(key, side).wait_send()
+
     for copy in ctrl_copies:
         copy.wait_send()
     for n in range(slices):
@@ -288,11 +343,10 @@
     def on_device(initial_state, capacity, source, control, segment_index):
         planes, rows, cols = initial_state.shape
         own_rows = rows // slices
-        reach = -(-(CORRECTIONS * SWEEPS + slices - CORRECTIONS) // 8) * 8
-        window = min(rows, own_rows + 2 * reach)
         fields = len(plan[0])
-        size = (planes, window, own_rows, reach, rows, cols, slices, count)
-        block = (planes, window, cols)
+        size = (planes, own_rows, rows, cols, slices, count)
+        block = (planes, own_rows, cols)
+        held = fields * ((planes + 2) * own_rows + 16 * planes) + (3 * slices + 3) * planes * own_rows
         dma = pltpu.SemaphoreType.DMA
         return pl.pallas_call(
             functools.partial(kernel, plan, size),
@@ -300,7 +354,8 @@
             in_specs=[pl.BlockSpec(memory_space=pl.ANY)] * 3 + [pl.BlockSpec(memory_space=pltpu.VMEM)] * 2,
             out_specs=pl.BlockSpec(memory_space=pl.ANY),
             scratch_shapes=[
-                pltpu.VMEM((fields, planes + 2, window, cols), jnp.float32),
+                pltpu.VMEM((fields, planes + 2, own_rows, cols), jnp.float32),
+                pltpu.VMEM((fields, 2, planes, 8, cols), jnp.float32),
                 pltpu.VMEM((slices,) + block, jnp.float32),
                 pltpu.VMEM((2 * slices,) + block, jnp.float32),
                 pltpu.VMEM(block, jnp.float32),
@@ -315,9 +370,11 @@
                 dma((slices,)),
                 dma((slices,)),
                 dma((2,)),
+                dma((fields, 2)),
+                dma((fields, 2)),
             ],
             compiler_params=pltpu.CompilerParams(
-                collective_id=0, has_side_effects=True, vmem_limit_bytes=67043328 - 1048576
+                collective_id=0, has_side_effects=True, vmem_limit_bytes=4 * cols * held + 3 * 1048576
             ),
         )(initial_state, capacity, source, control, segment_index)
 

time: 66 us -> 69.1 us (1.047); the launches traced: 65.8 us -> 67.8 us
  local copies, waits for them, and re-layouts: 1.87 us -> 5.25 us
  Pallas kernels: 63.9 us -> 62.6 us
    unnamed x1 -> x11, local copies, waits for them, and re-layouts: 1.87 us -> 5.25 us
    pallas_call x1, Pallas kernels: 63.9 us -> 62.6 us  [on_device(): pl.pallas_call(functools.partial(kernel, plan, size), out_shape=jax.Shape...]
where the time goes in v2:
time: 69.1 us; the launch traced here: 67.8 us
  Pallas kernels  62.6 us (91%)
  local copies, waits for them, and re-layouts  5.25 us (8%)
    pallas_call x1, Pallas kernels, on_device(): pl.pallas_call(functools.partial(kernel, plan, size), out_shape=jax.Shape...  62.6 us
    unnamed x11, local copies, waits for them, and re-layouts  5.25 us

profile of v2, /device:TPU:23, one launch (start us, length us, event | category | flops | bytes accessed | tf_op | source)
XLA Modules:
  0.0 67.8 jit_solution(13981022304099476262)
XLA Ops:
  0.0 0.0 copy-start
  0.0 1.0 %copy-done = f32[2,256,256]{2,1,0:T(8,128)S(1)} copy-done((f32[2,256,256]{2,1,0:T(8,128)S(1)}, f32[2,256,256]{2,1,0:T(8,128)}, u32[]{:S(2)}) %copy-start) | copy-done | bytes 524312
  1.0 0.0 copy-start.1
  1.0 1.0 %copy-done.1 = f32[2,256,256]{2,1,0:T(8,128)S(1)} copy-done((f32[2,256,256]{2,1,0:T(8,128)S(1)}, f32[2,256,256]{2,1,0:T(8,128)}, u32[]{:S(2)}) %copy-start.1) | copy-done | bytes 524312
  2.1 0.0 copy-start.2
  2.1 1.0 %copy-done.2 = f32[2,256,256]{2,1,0:T(8,128)S(1)} copy-done((f32[2,256,256]{2,1,0:T(8,128)S(1)}, f32[2,256,256]{2,1,0:T(8,128)}, u32[]{:S(2)}) %copy-start.2) | copy-done | bytes 524312
  3.1 0.0 copy-start.3
  3.1 0.7 %copy-done.3 = s32[2,256]{1,0:T(2,128)S(1)} copy-done((s32[2,256]{1,0:T(2,128)S(1)}, s32[2,256]{1,0:T(2,128)}, u32[]{:S(2)}) %copy-start.3) | copy-done | bytes 2072
  3.8 0.0 copy-start.4
  3.8 0.7 copy-done.4
  4.5 62.6 %shard_map.55 = f32[1,2,256,256]{3,2,1,0:T(8,128)S(1)} custom-call(f32[2,256,256]{2,1,0:T(8,128)S(1)} %copy-done, f32[2,256,256]{2,1,0:T(8,128)S(1)} %copy-done.1, f32[2,256,256]{2,1,0:T(8,128)S(1)} %copy-done.2, f32[1,16]{1,0:T(1,128)S(1)} %copy-done.4, s32[2,256]{1,0:T(2,128)S(1)} %copy-done.3), custom_call_target="tpu_custom_call" | custom-call | tf_op jit(solution)/shard_map/pallas_call | solution.py:351
  67.1 0.8 %copy.7 = f32[1,2,256,256]{3,2,1,0:T(8,128)} copy(f32[1,2,256,256]{3,2,1,0:T(8,128)S(1)} %shard_map.55) | data formatting | bytes 1048576
Async XLA Ops:
  0.0 1.0 %copy-start = (f32[2,256,256]{2,1,0:T(8,128)S(1)}, f32[2,256,256]{2,1,0:T(8,128)}, u32[]{:S(2)}) copy-start(f32[2,256,256]{2,1,0:T(8,128)} %state_hbm.1) | copy-start | bytes 1572868
  1.0 1.0 %copy-start.1 = (f32[2,256,256]{2,1,0:T(8,128)S(1)}, f32[2,256,256]{2,1,0:T(8,128)}, u32[]{:S(2)}) copy-start(f32[2,256,256]{2,1,0:T(8,128)} %cap_hbm.1) | copy-start | bytes 1572868
  2.1 1.0 %copy-start.2 = (f32[2,256,256]{2,1,0:T(8,128)S(1)}, f32[2,256,256]{2,1,0:T(8,128)}, u32[]{:S(2)}) copy-start(f32[2,256,256]{2,1,0:T(8,128)} %src_hbm.1) | copy-start | bytes 1572868
  3.1 0.7 %copy-start.3 = (s32[2,256]{1,0:T(2,128)S(1)}, s32[2,256]{1,0:T(2,128)}, u32[]{:S(2)}) copy-start(s32[2,256]{1,0:T(2,128)} %seg_ref.1) | copy-start | bytes 6148
  3.8 0.7 copy-start.4

commit v3 on v1

--- a/solution.py
+++ b/solution.py
@@ -102,21 +102,30 @@
             source_plane, target_plane, other = 1, planes + 1, s - 1
         else:
             source_plane, target_plane, other = planes, 0, s + 1
+        k, n, j = key
+        left = CORRECTIONS * (SWEEPS - 1) + slices - (k * (SWEEPS - 1) + n + j)
+        near = min(-(-left // 8) * 8, reach)
+        height = min(window, own_rows + 2 * near)
+        at = jnp.clip(t * own_rows - near, 0, rows - height) - first_row
+        needed = pl.ds(pl.multiple_of(at, 8), height)
         return pltpu.make_async_remote_copy(
-            src_ref=field.at[slot, source_plane],
-            dst_ref=field.at[slot, target_plane],
+            src_ref=field.at[slot, source_plane, needed],
+            dst_ref=field.at[slot, target_plane, needed],
             send_sem=send_sem.at[slot, side],
             recv_sem=recv_sem.at[slot, side],
             device_id={"space": other},
         )
 
-    def send(key):
+    odd = lax.rem(s, 2)
+
+    def send(key, parts=(0, 1)):
         if key in sent:
-            for side, there in ((0, low_there), (1, high_there)):
-
-                @pl.when(there)
-                def _():
-                    halo(key, side).start()
+            for part in parts:
+                for side, there in ((0, low_there), (1, high_there)):
+
+                    @pl.when(jnp.logical_and(there, odd == (side + part) % 2))
+                    def _():
+                        halo(key, side).start()
 
     arrived = set()
 
@@ -171,7 +180,10 @@
     step = window // 2 if window % 16 == 0 else window
     lane = lax.broadcasted_iota(jnp.int32, (step, cols), 1)
     line = lax.broadcasted_iota(jnp.int32, (step, cols), 0)
-    pieces = [(p, r) for p in range(planes) for r in range(0, window, step)]
+    pieces = []
+    for i in range(planes):
+        p = jnp.where(odd == 1, planes - 1 - i, i)
+        pieces += [(i, p, r) for r in range(0, window, step)]
 
     def neighbours(read, p, r):
         core = read(p + 1, r)
@@ -231,11 +243,13 @@
             if task[0] == "coarse":
                 _, n, source_key, target = task
                 arrive(source_key)
-                for p, r in pieces:
+                for i, p, r in pieces:
                     core, around = neighbours(reader(source_key), p, r)
                     field[slots[target], p + 1, pl.ds(r, step)] = core + piece(scale, p, r) * (
                         around - 6.0 * core + piece(forcing.at[n], p, r)
                     )
+                    if i == 0 and r + step == window:
+                        send(target, (0,))
             else:
                 _, n, source_key, target, j, pair = task
                 held = source_key[0] % 2 * slices + n
@@ -243,7 +257,7 @@
                 if pair is not None:
                     arrive(pair[0])
                     arrive(pair[1])
-                for p, r in pieces:
+                for i, p, r in pieces:
                     core, around = neighbours(reader(source_key), p, r)
                     gain = piece(inv, p, r)
                     if j == 1:
@@ -256,7 +270,9 @@
                         change, spread = neighbours(difference(*pair), p, r)
                         value = value + change + piece(scale, p, r) * (spread - 6.0 * change)
                     field[slots[target], p + 1, pl.ds(r, step)] = value
-            send(target)
+                    if i == 0 and r + step == window:
+                        send(target, (0,))
+            send(target, (1,))
             emit(target)
 
     for key in sorted(sent):

time: 66 us -> 63.5 us (0.962)
  Pallas kernels: 63.9 us -> 61.5 us
    pallas_call x1, Pallas kernels: 63.9 us -> 61.5 us  [on_device(): pl.pallas_call(functools.partial(kernel, plan, size), out_shape=jax.Shape...]
where the time goes in v3:
time: 63.5 us; the launch traced here: 63.3 us
  Pallas kernels  61.5 us (97%)
  local copies, waits for them, and re-layouts  1.87 us (3%)
    pallas_call x1, Pallas kernels, on_device(): pl.pallas_call(functools.partial(kernel, plan, size), out_shape=jax.Shape...  61.5 us
    unnamed x1, local copies, waits for them, and re-layouts  1.87 us

profile of v3, /device:TPU:23, one launch (start us, length us, event | category | flops | bytes accessed | tf_op | source)
XLA Modules:
  0.0 63.3 jit_solution(13040109496753370785)
XLA Ops:
  0.0 61.5 %shard_map.55 = f32[1,2,256,256]{3,2,1,0:T(8,128)} custom-call(f32[2,256,256]{2,1,0:T(8,128)} %state_hbm.1, f32[2,256,256]{2,1,0:T(8,128)} %cap_hbm.1, f32[2,256,256]{2,1,0:T(8,128)} %src_hbm.1, f32[1,16]{1,0:T(1,128)} %ctrl_ref.1, s32[2,256]{1,0:T(2,128)} %seg_ref.1), custom_call_target="tpu_custom_call" | custom-call | tf_op jit(solution)/shard_map/pallas_call | solution.py:313
  61.5 1.9 %copy.7 = f32[1,2,256,256]{3,2,1,0:T(8,128)} copy(f32[1,2,256,256]{3,2,1,0:T(8,128)} %shard_map.55) | data formatting | bytes 1048576
